TPU v7x, 128 devices: a whole 4x4x4 slice. The times are simulated.
128 devices in a mesh: gy: 2 (over core), gx: 64 (over z, y, x).
Axes of the slice: x: 4, y: 4, z: 4, core: 2. Of those that a mesh axis runs over, the one named last changes fastest.
Arguments:
- basis_vectors: float32 [36, 256, 128, 256], P(None, 'gx', 'gy'), may hold values from -30 to 30, as said below
- reaction: float32 [256, 128, 256], P('gx', 'gy'), may hold values from 0.5 to 3
Outputs:
- new_vectors: float32 [4, 256, 128, 256], P(None, 'gx', 'gy')
- hessenberg: float32 [40, 4], replicated
Inputs may be any that keep to these rules, and one draw needn't show every extreme that they name: `basis_vectors`: under the inner product the basis vectors are nearly orthonormal.
All inputs are finite; a program needn't handle non-finite values.
Results may differ from a plain program's by a relative error of at most 0.0003.
Values sent between devices are 32-bit elements; how exact they have to be, the bound alone decides.
A program may use at most 128 MiB of HBM per device.

v0:
```python
import jax
import jax.numpy as jnp
from jax import lax
from jax.sharding import Mesh
from jax.sharding import PartitionSpec as P

STEPS = 4
GX = ("gx_0", "gx_1", "gx_2")


WIND_SPEEDS = (0.9, 0.6, 0.4)
EPSILON = 1e-06


def shifted(block, axis, distance):
    devices = range(lax.axis_size(axis))
    route = [(i - distance, i) for i in devices if i - distance in devices]
    return lax.ppermute(block, axis, route)


def copy_for_each(array, axis):
    copies = jnp.broadcast_to(array, (lax.axis_size(axis), *array.shape))
    return lax.all_to_all(copies, axis, split_axis=0, concat_axis=0, tiled=True)


def over_copies(array, axis):
    everything = copy_for_each(array, axis)
    return jnp.sum(everything, axis=0)


def by_axis(array, axes):
    far, near = axes
    nearer = over_copies(array, near)
    return over_copies(nearer, far)


def in_one(arrays, axis):
    ends = [0]
    for a in arrays:
        ends.append(ends[-1] + a.size)
    running = by_axis(jnp.concatenate([a.ravel() for a in arrays]), axis)
    return tuple((running[b:e].reshape(a.shape) for a, b, e in zip(arrays, ends, ends[1:])))


def stencil(values, x_ext, y_ext, z_ext, reaction):
    summed = -reaction * values
    for position, extended in enumerate((x_ext, y_ext, z_ext)):
        count = values.shape[position]
        higher = lax.slice_in_dim(extended, 3, count + 3, axis=position)
        lower_one = lax.slice_in_dim(extended, 1, count + 1, axis=position)
        lower_two = lax.slice_in_dim(extended, 0, count, axis=position)
        wind_speed = WIND_SPEEDS[position]
        summed = (
            summed
            + higher
            + lower_one
            - 2.0 * values
            - wind_speed * (3.0 * values - 4.0 * lower_one + lower_two) * 0.5
        )
    return summed


def apply_operator(values, reaction):
    rows_x = values.shape[0]
    rows_y = values.shape[1]
    lower_x = shifted(values[rows_x - 2 :], GX, 1)
    upper_x = shifted(values[:1], GX, -1)
    lower_y = shifted(values[:, rows_y - 2 :], "gy", 1)
    upper_y = shifted(values[:, :1], "gy", -1)
    x_ext = jnp.concatenate([lower_x, values, upper_x], axis=0)
    y_ext = jnp.concatenate([lower_y, values, upper_y], axis=1)
    z_ext = jnp.pad(values, ((0, 0), (0, 0), (2, 1)))
    return stencil(values, x_ext, y_ext, z_ext, reaction)


def project(basis_vectors, created, image):
    local = jnp.einsum("kxyz,xyz->k", basis_vectors, image, precision=lax.Precision.HIGHEST)
    extra = [jnp.sum(vector * image)[None] for vector in created]
    return jnp.concatenate([local] + extra)


def combine(basis_vectors, created, weights):
    keep_count = basis_vectors.shape[0]
    summed = jnp.einsum(
        "k,kxyz->xyz", weights[:keep_count], basis_vectors, precision=lax.Precision.HIGHEST
    )
    for index, vector in enumerate(created):
        summed = summed + weights[keep_count + index] * vector
    return summed


def body(basis_vectors, reaction):
    keep_count = basis_vectors.shape[0]
    basis_size = keep_count + STEPS
    cell_count = float(
        basis_vectors.shape[1]
        * basis_vectors.shape[2]
        * basis_vectors.shape[3]
        * lax.axis_size(GX)
        * lax.axis_size("gy")
    )
    created = []
    columns = []
    local_gram = jnp.einsum(
        "axyz,bxyz->ab", basis_vectors, basis_vectors, precision=lax.Precision.HIGHEST
    )
    kept_gram = by_axis(local_gram, ("gy", ("gx_0", "gx_1", "gx_2"))) / cell_count
    gram_matrix = (
        jnp.zeros((basis_size, basis_size), jnp.float32).at[:keep_count, :keep_count].set(kept_gram)
    )
    for section in range(STEPS):
        current = keep_count + section
        vector_now = basis_vectors[keep_count - 1] if section == 0 else created[-1]
        image = apply_operator(vector_now, reaction)
        first_terms = (
            by_axis(project(basis_vectors, created, image), ("gy", ("gx_0", "gx_1", "gx_2")))
            / cell_count
        )
        first_rest = image - combine(basis_vectors, created, first_terms)
        second_terms, rest_square = in_one(
            (project(basis_vectors, created, first_rest), jnp.sum(first_rest * first_rest)),
            ("gy", ("gx_0", "gx_1", "gx_2")),
        )
        second_terms = second_terms / cell_count
        rest_square = rest_square / cell_count
        gram_now = gram_matrix[:current, :current]
        folded = jnp.dot(gram_now, second_terms, precision=lax.Precision.HIGHEST)
        second_rest = first_rest - combine(basis_vectors, created, second_terms)
        squared = (
            rest_square
            - 2.0 * jnp.sum(second_terms * second_terms)
            + jnp.sum(second_terms * folded)
        )
        length_now = jnp.sqrt(squared + EPSILON)
        cross_terms = (second_terms - folded) / length_now
        gram_matrix = gram_matrix.at[:current, current].set(cross_terms)
        gram_matrix = gram_matrix.at[current, :current].set(cross_terms)
        gram_matrix = gram_matrix.at[current, current].set(squared / (length_now * length_now))
        weights = first_terms + second_terms
        columns.append(
            jnp.concatenate(
                [weights, length_now[None], jnp.zeros((basis_size - current - 1,), jnp.float32)]
            )
        )
        created.append(second_rest / length_now)
    return (jnp.stack(created), jnp.stack(columns, axis=1))


def solution(mesh):
    split = Mesh(mesh.devices.reshape(mesh.shape["gy"], 4, 4, 4), ("gy", "gx_0", "gx_1", "gx_2"))
    placed = (P(None, GX, "gy", None), P(GX, "gy", None))
    return jax.shard_map(
        body, mesh=split, in_specs=placed, out_specs=(P(None, GX, "gy", None), P()), check_vma=False
    )
```

profile of v0, /device:TPU:1, one launch (start us, length us, event | category | flops | bytes accessed | tf_op | source)
XLA Modules:
  0.0 552.3 jit_solution(16492750439540442998)
XLA Ops:
  13.6 25.8 %fusion.34 = f32[36,36]{1,0:T(8,128)S(1)} fusion(f32[36,4,64,256]{3,2,1,0:T(8,128)} %param.22), kind=kOutput, calls=%fused_computation.34 | convolution fusion | flops 1019215872 | bytes 9442368 | tf_op jit(solution)/shard_map/axyz,bxyz->ab/dot_general | solution.py:104
  41.9 13.0 %fusion.38 = f32[36]{0:T(128)S(1)} fusion(f32[36,4,64,256]{3,2,1,0:T(8,128)S(1)} %copy-done, f32[4,64,256,1]{2,1,0,3:T(8,128)S(1)} %bitcast.255), kind=kOutput, calls=%fused_computation.40 | convolution fusion | flops 28311552 | bytes 9699472 | tf_op jit(solution)/shard_map/kxyz,xyz->k/dot_general | solution.py:77
  55.5 12.0 %all-to-all-start = ((f32[64,1,36]{2,1,0:T(1,128)}), f32[64,1,36]{2,1,0:T(1,128)S(1)}, u32[]{:S(2)}, u32[]{:S(2)}) async-start(f32[64,1,36]{2,1,0:T(1,128)} %broadcast_in_dim.103), calls=%async_computation | async-start | bytes 65536 | tf_op jit(solution)/shard_map/all_to_all | solution.py:23
  68.1 7.8 %all-to-all-done = f32[64,1,36]{2,1,0:T(1,128)S(1)} async-done(((f32[64,1,36]{2,1,0:T(1,128)}), f32[64,1,36]{2,1,0:T(1,128)S(1)}, u32[]{:S(2)}, u32[]{:S(2)}) %all-to-all-start) | async-done | bytes 9248 | tf_op jit(solution)/shard_map/all_to_all | solution.py:23
  80.7 14.5 %fusion.26 = f32[1,4,64,256]{3,0,2,1:T(1,128)S(1)} fusion(f32[36,4,64,256]{3,2,1,0:T(8,128)} %param.22, f32[36]{0:T(128)S(1)} %reduce_sum.379), kind=kOutput, calls=%fused_computation.26 | convolution fusion | flops 28311588 | bytes 9699472 | tf_op jit(solution)/shard_map/k,kxyz->xyz/dot_general | solution.py:84
  95.9 16.0 %fusion.41 = f32[36]{0:T(128)S(1)} fusion(f32[36,4,64,256]{3,2,1,0:T(8,128)} %param.22, f32[4,64,256,1]{2,1,0,3:T(8,128)S(1)} %get-tuple-element.149), kind=kOutput, calls=%fused_computation.41 | convolution fusion | flops 28311552 | bytes 9699472 | tf_op jit(solution)/shard_map/kxyz,xyz->k/dot_general | solution.py:77
  137.8 14.5 %fusion.22 = f32[1,4,64,256]{3,0,2,1:T(1,128)S(1)} fusion(f32[36,4,64,256]{3,2,1,0:T(8,128)} %param.22, f32[37]{0:T(128)S(1)} %reduce_sum.382), kind=kOutput, calls=%fused_computation.22 | convolution fusion | flops 28311588 | bytes 9699476 | tf_op jit(solution)/shard_map/k,kxyz->xyz/dot_general | solution.py:84
  172.9 16.3 %fusion.44 = f32[36]{0:T(128)S(1)} fusion(f32[36,4,64,256]{3,2,1,0:T(8,128)} %param.22, f32[4,64,256,1]{2,1,0,3:T(8,128)S(1)} %bitcast.258), kind=kOutput, calls=%fused_computation.42 | convolution fusion | flops 28311552 | bytes 9699472 | tf_op jit(solution)/shard_map/kxyz,xyz->k/dot_general | solution.py:77
  190.6 11.9 %all-to-all-start.6 = ((f32[64,1,37]{2,1,0:T(1,128)}), f32[64,1,37]{2,1,0:T(1,128)S(1)}, u32[]{:S(2)}, u32[]{:S(2)}) async-start(f32[64,1,37]{2,1,0:T(1,128)} %broadcast_in_dim.110), calls=%async_computation.6 | async-start | bytes 65536 | tf_op jit(solution)/shard_map/all_to_all | solution.py:23
  202.6 8.2 %all-to-all-done.6 = f32[64,1,37]{2,1,0:T(1,128)S(1)} async-done(((f32[64,1,37]{2,1,0:T(1,128)}), f32[64,1,37]{2,1,0:T(1,128)S(1)}, u32[]{:S(2)}, u32[]{:S(2)}) %all-to-all-start.6) | async-done | bytes 9504 | tf_op jit(solution)/shard_map/all_to_all | solution.py:23
  217.5 14.6 %fusion.18 = f32[1,4,64,256]{3,0,2,1:T(1,128)S(1)} fusion(f32[36,4,64,256]{3,2,1,0:T(8,128)} %param.22, f32[37]{0:T(128)S(1)} %broadcast_multiply_fusion.3), kind=kOutput, calls=%fused_computation.18 | convolution fusion | flops 28311552 | bytes 9699476 | tf_op jit(solution)/shard_map/k,kxyz->xyz/dot_general | solution.py:84
  234.1 16.0 %fusion.47 = f32[36]{0:T(128)S(1)} fusion(f32[36,4,64,256]{3,2,1,0:T(8,128)} %param.22, f32[4,64,256,1]{2,1,0,3:T(8,128)S(1)} %bitcast.256), kind=kOutput, calls=%fused_computation.43 | convolution fusion | flops 28311552 | bytes 9699472 | tf_op jit(solution)/shard_map/kxyz,xyz->k/dot_general | solution.py:77
  273.8 14.7 %fusion.14 = f32[1,4,64,256]{3,0,2,1:T(1,128)S(1)} fusion(f32[36,4,64,256]{3,2,1,0:T(8,128)} %param.22, f32[37]{0:T(128)S(1)} %get-tuple-element.172), kind=kOutput, calls=%fused_computation.14 | convolution fusion | flops 28311552 | bytes 9699476 | tf_op jit(solution)/shard_map/k,kxyz->xyz/dot_general | solution.py:84
  300.2 16.3 %fusion.50 = f32[36]{0:T(128)S(1)} fusion(f32[36,4,64,256]{3,2,1,0:T(8,128)} %param.22, f32[4,64,256,1]{2,1,0,3:T(8,128)S(1)} %bitcast.261), kind=kOutput, calls=%fused_computation.44 | convolution fusion | flops 28311552 | bytes 9699472 | tf_op jit(solution)/shard_map/kxyz,xyz->k/dot_general | solution.py:77
  318.5 10.9 %all-to-all-start.10 = ((f32[64,1,38]{2,1,0:T(1,128)}), f32[64,1,38]{2,1,0:T(1,128)S(1)}, u32[]{:S(2)}, u32[]{:S(2)}) async-start(f32[64,1,38]{2,1,0:T(1,128)} %broadcast_in_dim.117), calls=%async_computation.10 | async-start | bytes 65536 | tf_op jit(solution)/shard_map/all_to_all | solution.py:23
  330.1 7.6 %all-to-all-done.10 = f32[64,1,38]{2,1,0:T(1,128)S(1)} async-done(((f32[64,1,38]{2,1,0:T(1,128)}), f32[64,1,38]{2,1,0:T(1,128)S(1)}, u32[]{:S(2)}, u32[]{:S(2)}) %all-to-all-start.10) | async-done | bytes 9760 | tf_op jit(solution)/shard_map/all_to_all | solution.py:23
  344.4 14.6 %fusion.10 = f32[1,4,64,256]{3,0,2,1:T(1,128)S(1)} fusion(f32[36,4,64,256]{3,2,1,0:T(8,128)} %param.22, f32[38]{0:T(128)S(1)} %broadcast_multiply_fusion.2), kind=kOutput, calls=%fused_computation.10 | convolution fusion | flops 28311552 | bytes 9699480 | tf_op jit(solution)/shard_map/k,kxyz->xyz/dot_general | solution.py:84
  361.8 16.0 %fusion.53 = f32[36]{0:T(128)S(1)} fusion(f32[36,4,64,256]{3,2,1,0:T(8,128)} %param.22, f32[4,64,256,1]{2,1,0,3:T(8,128)S(1)} %bitcast.260), kind=kOutput, calls=%fused_computation.45 | convolution fusion | flops 28311552 | bytes 9699472 | tf_op jit(solution)/shard_map/kxyz,xyz->k/dot_general | solution.py:77
  402.1 14.7 %fusion.6 = f32[1,4,64,256]{3,0,2,1:T(1,128)S(1)} fusion(f32[36,4,64,256]{3,2,1,0:T(8,128)} %param.22, f32[38]{0:T(128)S(1)} %get-tuple-element.163), kind=kOutput, calls=%fused_computation.6 | convolution fusion | flops 28311552 | bytes 9699480 | tf_op jit(solution)/shard_map/k,kxyz->xyz/dot_general | solution.py:84
  428.6 16.3 %fusion.56 = f32[36]{0:T(128)S(1)} fusion(f32[36,4,64,256]{3,2,1,0:T(8,128)} %param.22, f32[4,64,256,1]{2,1,0,3:T(8,128)S(1)} %bitcast.257), kind=kOutput, calls=%fused_computation.46 | convolution fusion | flops 28311552 | bytes 9699472 | tf_op jit(solution)/shard_map/kxyz,xyz->k/dot_general | solution.py:77
  447.5 10.8 %all-to-all-start.14 = ((f32[64,1,39]{2,1,0:T(1,128)}), f32[64,1,39]{2,1,0:T(1,128)S(1)}, u32[]{:S(2)}, u32[]{:S(2)}) async-start(f32[64,1,39]{2,1,0:T(1,128)} %broadcast_in_dim.126), calls=%async_computation.14 | async-start | bytes 65536 | tf_op jit(solution)/shard_map/all_to_all | solution.py:23
  473.4 14.6 %fusion.2 = f32[1,4,64,256]{3,0,2,1:T(1,128)S(1)} fusion(f32[36,4,64,256]{3,2,1,0:T(8,128)} %param.22, f32[39]{0:T(128)S(1)} %broadcast_multiply_fusion.1), kind=kOutput, calls=%fused_computation.2 | convolution fusion | flops 28311552 | bytes 9699484 | tf_op jit(solution)/shard_map/k,kxyz->xyz/dot_general | solution.py:84
  491.5 16.0 %fusion.59 = f32[36]{0:T(128)S(1)} fusion(f32[36,4,64,256]{3,2,1,0:T(8,128)} %param.22, f32[4,64,256,1]{2,1,0,3:T(8,128)S(1)} %bitcast.259), kind=kOutput, calls=%fused_computation.47 | convolution fusion | flops 28311552 | bytes 9699472 | tf_op jit(solution)/shard_map/kxyz,xyz->k/dot_general | solution.py:77
  530.1 14.7 %fusion.28 = f32[1,4,64,256]{3,0,2,1:T(1,128)S(1)} fusion(f32[36,4,64,256]{3,2,1,0:T(8,128)} %param.22, f32[39]{0:T(128)S(1)} %get-tuple-element.156), kind=kOutput, calls=%fused_computation.28 | convolution fusion | flops 28311552 | bytes 9699484 | tf_op jit(solution)/shard_map/k,kxyz->xyz/dot_general | solution.py:84
  (196 shorter events, 204.7 us)
Async XLA Ops:
  1.8 39.6 %collective-permute-start.3 = (f32[4,2,256]{2,1,0:T(2,128)S(1)}, f32[4,2,256]{2,1,0:T(2,128)S(1)}, u32[]{:S(2)}, u32[]{:S(2)}) collective-permute-start(f32[4,2,256]{2,1,0:T(2,128)S(1)} %slice.566), channel_id=1, source_target_pairs={{0,64},{1,65},{2,66},{3,67},{4,68},{5,69},{6,70},{7,71},{8,72},{9,... | collective-permute-start | bytes 24584 | tf_op jit(solution)/shard_map/ppermute | solution.py:18
  3.4 38.0 %collective-permute-start.2 = (f32[4,1,256]{2,1,0:T(1,128)S(1)}, f32[4,1,256]{2,1,0:T(1,128)S(1)}, u32[]{:S(2)}, u32[]{:S(2)}) collective-permute-start(f32[4,1,256]{2,1,0:T(1,128)S(1)} %slice.565), channel_id=1, source_target_pairs={{64,0},{65,1},{66,2},{67,3},{68,4},{69,5},{70,6},{71,7},{72,8},{73... | collective-permute-start | bytes 12296 | tf_op jit(solution)/shard_map/ppermute | solution.py:18
  7.8 33.7 %collective-permute-start.1 = (f32[2,64,256]{2,1,0:T(8,128)S(1)}, f32[2,64,256]{2,1,0:T(8,128)S(1)}, u32[]{:S(2)}, u32[]{:S(2)}) collective-permute-start(f32[2,64,256]{2,1,0:T(8,128)S(1)} %slice_bitcast_fusion.1), channel_id=1, source_target_pairs={{0,1},{1,2},{2,3},{3,4},{4,5},{5,6},{6,7},{7,8},{8,9},{9,10},{10,1... | collective-permute-start | bytes 393224 | tf_op jit(solution)/shard_map/ppermute | solution.py:18
  12.3 29.2 %collective-permute-start = (f32[1,64,256]{2,1,0:T(8,128)S(1)}, f32[1,64,256]{2,1,0:T(8,128)S(1)}, u32[]{:S(2)}, u32[]{:S(2)}) collective-permute-start(f32[1,64,256]{2,1,0:T(8,128)S(1)} %slice_bitcast_fusion.2), channel_id=1, source_target_pairs={{1,0},{2,1},{3,2},{4,3},{5,4},{6,5},{7,6},{8,7},{9,8},{10,9},{11,1... | collective-permute-start | bytes 196616 | tf_op jit(solution)/shard_map/ppermute | solution.py:18
  55.5 20.4 %all-to-all-start = ((f32[64,1,36]{2,1,0:T(1,128)}), f32[64,1,36]{2,1,0:T(1,128)S(1)}, u32[]{:S(2)}, u32[]{:S(2)}) async-start(f32[64,1,36]{2,1,0:T(1,128)} %broadcast_in_dim.103), calls=%async_computation | async-start | bytes 65536 | tf_op jit(solution)/shard_map/all_to_all | solution.py:23
  113.3 13.1 %all-to-all-start.2 = ((f32[64,1,37]{2,1,0:T(1,128)}), f32[64,1,37]{2,1,0:T(1,128)S(1)}, u32[]{:S(2)}, u32[]{:S(2)}) async-start(f32[64,1,37]{2,1,0:T(1,128)} %broadcast_in_dim.105), calls=%async_computation.2 | async-start | bytes 65536 | tf_op jit(solution)/shard_map/all_to_all | solution.py:23
  131.5 20.7 %all-to-all-start.4 = ((f32[64,1,1296]{2,1,0:T(1,128)}), f32[64,1,1296]{2,1,0:T(1,128)S(1)}, u32[]{:S(2)}, u32[]{:S(2)}) async-start(f32[64,1,1296]{2,1,0:T(1,128)} %reshape.447), calls=%async_computation.4 | async-start | bytes 720896 | tf_op jit(solution)/shard_map/all_to_all | solution.py:23
  162.2 9.8 %collective-permute-start.5 = (f32[2,64,256]{2,1,0:T(8,128)S(1)}, f32[2,64,256]{2,1,0:T(8,128)S(1)}, u32[]{:S(2)}, u32[]{:S(2)}) collective-permute-start(f32[2,64,256]{2,1,0:T(8,128)S(1)} %slice.570), channel_id=1, source_target_pairs={{0,1},{1,2},{2,3},{3,4},{4,5},{5,6},{6,7},{7,8},{8,9},{9,10},{10,1... | collective-permute-start | bytes 393224 | tf_op jit(solution)/shard_map/ppermute | solution.py:18
  165.5 6.4 %collective-permute-start.4 = (f32[1,64,256]{2,1,0:T(8,128)S(1)}, f32[1,64,256]{2,1,0:T(8,128)S(1)}, u32[]{:S(2)}, u32[]{:S(2)}) collective-permute-start(f32[1,64,256]{2,1,0:T(8,128)S(1)} %slice.569), channel_id=1, source_target_pairs={{1,0},{2,1},{3,2},{4,3},{5,4},{6,5},{7,6},{8,7},{9,8},{10,9},{11,1... | collective-permute-start | bytes 196616 | tf_op jit(solution)/shard_map/ppermute | solution.py:18
  166.8 5.1 collective-permute-start.7
  168.1 3.8 collective-permute-start.6
  190.6 20.2 %all-to-all-start.6 = ((f32[64,1,37]{2,1,0:T(1,128)}), f32[64,1,37]{2,1,0:T(1,128)S(1)}, u32[]{:S(2)}, u32[]{:S(2)}) async-start(f32[64,1,37]{2,1,0:T(1,128)} %broadcast_in_dim.110), calls=%async_computation.6 | async-start | bytes 65536 | tf_op jit(solution)/shard_map/all_to_all | solution.py:23
  252.1 13.0 %all-to-all-start.8 = ((f32[64,1,38]{2,1,0:T(1,128)}), f32[64,1,38]{2,1,0:T(1,128)S(1)}, u32[]{:S(2)}, u32[]{:S(2)}) async-start(f32[64,1,38]{2,1,0:T(1,128)} %broadcast_in_dim.113), calls=%async_computation.8 | async-start | bytes 65536 | tf_op jit(solution)/shard_map/all_to_all | solution.py:23
  289.8 9.3 %collective-permute-start.9 = (f32[2,64,256]{2,1,0:T(8,128)S(1)}, f32[2,64,256]{2,1,0:T(8,128)S(1)}, u32[]{:S(2)}, u32[]{:S(2)}) collective-permute-start(f32[2,64,256]{2,1,0:T(8,128)S(1)} %slice.579), channel_id=1, source_target_pairs={{0,1},{1,2},{2,3},{3,4},{4,5},{5,6},{6,7},{7,8},{8,9},{9,10},{10,1... | collective-permute-start | bytes 393224 | tf_op jit(solution)/shard_map/ppermute | solution.py:18
  292.6 6.4 %collective-permute-start.8 = (f32[1,64,256]{2,1,0:T(8,128)S(1)}, f32[1,64,256]{2,1,0:T(8,128)S(1)}, u32[]{:S(2)}, u32[]{:S(2)}) collective-permute-start(f32[1,64,256]{2,1,0:T(8,128)S(1)} %slice.578), channel_id=1, source_target_pairs={{1,0},{2,1},{3,2},{4,3},{5,4},{6,5},{7,6},{8,7},{9,8},{10,9},{11,1... | collective-permute-start | bytes 196616 | tf_op jit(solution)/shard_map/ppermute | solution.py:18
  293.9 5.1 collective-permute-start.11
  295.2 3.8 collective-permute-start.10
  318.5 19.2 %all-to-all-start.10 = ((f32[64,1,38]{2,1,0:T(1,128)}), f32[64,1,38]{2,1,0:T(1,128)S(1)}, u32[]{:S(2)}, u32[]{:S(2)}) async-start(f32[64,1,38]{2,1,0:T(1,128)} %broadcast_in_dim.117), calls=%async_computation.10 | async-start | bytes 65536 | tf_op jit(solution)/shard_map/all_to_all | solution.py:23
  380.4 13.0 %all-to-all-start.12 = ((f32[64,1,39]{2,1,0:T(1,128)}), f32[64,1,39]{2,1,0:T(1,128)S(1)}, u32[]{:S(2)}, u32[]{:S(2)}) async-start(f32[64,1,39]{2,1,0:T(1,128)} %broadcast_in_dim.121), calls=%async_computation.12 | async-start | bytes 65536 | tf_op jit(solution)/shard_map/all_to_all | solution.py:23
  418.8 8.8 %collective-permute-start.13 = (f32[2,64,256]{2,1,0:T(8,128)S(1)}, f32[2,64,256]{2,1,0:T(8,128)S(1)}, u32[]{:S(2)}, u32[]{:S(2)}) collective-permute-start(f32[2,64,256]{2,1,0:T(8,128)S(1)} %slice.588), channel_id=1, source_target_pairs={{0,1},{1,2},{2,3},{3,4},{4,5},{5,6},{6,7},{7,8},{8,9},{9,10},{10,1... | collective-permute-start | bytes 393224 | tf_op jit(solution)/shard_map/ppermute | solution.py:18
  421.1 6.4 %collective-permute-start.12 = (f32[1,64,256]{2,1,0:T(8,128)S(1)}, f32[1,64,256]{2,1,0:T(8,128)S(1)}, u32[]{:S(2)}, u32[]{:S(2)}) collective-permute-start(f32[1,64,256]{2,1,0:T(8,128)S(1)} %slice.587), channel_id=1, source_target_pairs={{1,0},{2,1},{3,2},{4,3},{5,4},{6,5},{7,6},{8,7},{9,8},{10,9},{11,1... | collective-permute-start | bytes 196616 | tf_op jit(solution)/shard_map/ppermute | solution.py:18
  422.4 5.1 collective-permute-start.15
  447.5 19.2 %all-to-all-start.14 = ((f32[64,1,39]{2,1,0:T(1,128)}), f32[64,1,39]{2,1,0:T(1,128)S(1)}, u32[]{:S(2)}, u32[]{:S(2)}) async-start(f32[64,1,39]{2,1,0:T(1,128)} %broadcast_in_dim.126), calls=%async_computation.14 | async-start | bytes 65536 | tf_op jit(solution)/shard_map/all_to_all | solution.py:23
  510.7 13.0 %all-to-all-start.16 = ((f32[64,1,40]{2,1,0:T(1,128)}), f32[64,1,40]{2,1,0:T(1,128)S(1)}, u32[]{:S(2)}, u32[]{:S(2)}) async-start(f32[64,1,40]{2,1,0:T(1,128)} %broadcast_in_dim.131), calls=%async_computation.16 | async-start | bytes 65536 | tf_op jit(solution)/shard_map/all_to_all | solution.py:23
  (6 other events, 204.2 us)
where the time goes:
time: 562 us; the launch traced here: 552 us
  matrix products  272 us (48%)
  starting transfers between devices  104 us (19%)
  waiting for transfers between devices  53.9 us (10%)
  blocking collectives  48.8 us (9%)
  other arithmetic  36.2 us (6%)
  local copies, waits for them, and re-layouts  28 us (5%)
  between operations  9.69 us (2%)
    dot_general x8, matrix products, project(): jnp.einsum('kxyz,xyz->k', basis_vectors, image, precision=lax.Precision.H...  126 us
    dot_general x8, matrix products, combine(): jnp.einsum('k,kxyz->xyz', weights[:keep_count], basis_vectors, precision=...  117 us
    all_to_all x9, starting transfers between devices, copy_for_each(): return lax.all_to_all(copies, axis, split_axis=0, concat_axis=0, tiled=True)  69.3 us
    all_to_all x9, waiting for transfers between devices, copy_for_each(): return lax.all_to_all(copies, axis, split_axis=0, concat_axis=0, tiled=True)  51.6 us
    all_to_all x9, blocking collectives, copy_for_each(): return lax.all_to_all(copies, axis, split_axis=0, concat_axis=0, tiled=True)  48.8 us
    ppermute x16, starting transfers between devices, shifted(): return lax.ppermute(block, axis, route)  34.5 us
    dot_general x1, matrix products, body(): jnp.einsum('axyz,bxyz->ab', basis_vectors, basis_vectors, precision=lax.P...  25.8 us
  transfers between devices with their start and end apart: 25, of which 11 were waited for; matrix products, arithmetic and copies ran while one was open for 11% of the time, Pallas kernels for 0%

commit v1 on v0

v1 whole, which is shorter than its diff:
```python
import functools

import jax
import jax.numpy as jnp
from jax import lax
from jax.experimental import pallas as pl
from jax.experimental.pallas import tpu as pltpu
from jax.sharding import PartitionSpec as P

MESH = pl.DeviceIdType.MESH
STEPS = 4
WIND = (0.9, 0.6, 0.4)
EPSILON = 1e-06
SIDE = 4
CHIPS = 64
DEVICES = 128
ROWS = 40


def hops(delta):
    return sum(min(d, SIDE - d) for d in delta[:3])


def partners(with_core):
    places = [
        (z, y, x, c)
        for z in range(SIDE)
        for y in range(SIDE)
        for x in range(SIDE)
        for c in range(2 if with_core else 1)
    ]
    return sorted(
        [p for p in places if any(p)], key=lambda p: (-hops(p), p[2], p[1], p[0])
    )


def kernel(
    keep,
    planes,
    rows,
    cols,
    basis,
    react,
    out,
    hess,
    V,
    W,
    RC,
    low_x,
    high_x,
    side_y,
    acc,
    acc_kept,
    gram_hh,
    gram_hl,
    gram_ll,
    hb,
    row_src,
    row_all,
    pair_src,
    pair_got,
    half_src,
    half_all,
    half_got,
    load_sem,
    x_send,
    low_recv,
    high_recv,
    y_send,
    y_recv,
    row_send,
    row_recv,
    gram_send,
    gram_recv,
):
    f32 = jnp.float32
    core = lax.axis_index("gy")
    chip = lax.axis_index("gx")
    me = core * CHIPS + chip
    cz, cy, cx = lax.div(chip, 16), lax.rem(lax.div(chip, 4), 4), lax.rem(chip, 4)
    zs = [lax.rem(cz + d, SIDE) * 16 for d in range(SIDE)]
    ys = [lax.rem(cy + d, SIDE) * 4 for d in range(SIDE)]
    xs = [lax.rem(cx + d, SIDE) for d in range(SIDE)]
    cores = [core, 1 - core]
    inv_cells = 1.0 / float(DEVICES * planes * rows * cols)

    def device(place):
        z, y, x, c = place
        return {"gy": cores[c], "gx": zs[z] + ys[y] + xs[x]}

    barrier = pltpu.get_barrier_semaphore()
    for place in partners(True):
        pl.semaphore_signal(
            barrier, inc=1, device_id=device(place), device_id_type=MESH
        )

    last = keep - 1
    loads = [
        pltpu.make_async_copy(basis.at[last], V.at[last], load_sem.at[0]),
        pltpu.make_async_copy(react, RC, load_sem.at[1]),
    ]
    for n, start in enumerate(range(0, last, 7)):
        part = pl.ds(start, min(7, last - start))
        loads.append(
            pltpu.make_async_copy(basis.at[part], V.at[part], load_sem.at[2 + n])
        )
    for copy in loads:
        copy.start()

    acc[...] = jnp.zeros(acc.shape, f32)
    acc_kept[...] = jnp.zeros(acc_kept.shape, f32)
    gram_hh[...] = jnp.zeros(gram_hh.shape, f32)
    gram_hl[...] = jnp.zeros(gram_hl.shape, f32)
    gram_ll[...] = jnp.zeros(gram_ll.shape, f32)

    @pl.when(chip == 0)
    def _():
        low_x[...] = jnp.zeros(low_x.shape, f32)

    @pl.when(chip == CHIPS - 1)
    def _():
        high_x[...] = jnp.zeros(high_x.shape, f32)

    loads[0].wait()
    pl.semaphore_wait(barrier, DEVICES - 1)

    def to_next(step, plane):
        return pltpu.make_async_remote_copy(
            V.at[last + step, plane],
            low_x.at[step, plane - (planes - 2)],
            x_send.at[step, plane - (planes - 2)],
            low_recv.at[step, plane - (planes - 2)],
            device_id={"gy": core, "gx": lax.rem(chip + 1, CHIPS)},
            device_id_type=MESH,
        )

    def to_previous(step):
        return pltpu.make_async_remote_copy(
            V.at[last + step, 0],
            high_x.at[step],
            x_send.at[step, 2],
            high_recv.at[step],
            device_id={"gy": core, "gx": lax.rem(chip + CHIPS - 1, CHIPS)},
            device_id_type=MESH,
        )

    edge = pl.ds(pl.multiple_of((1 - core) * (rows - 8), 8), 8)

    def to_side(step, plane):
        return pltpu.make_async_remote_copy(
            V.at[last + step, plane, edge],
            side_y.at[step, plane],
            y_send.at[step, plane],
            y_recv.at[step, plane],
            device_id={"gy": 1 - core, "gx": chip},
            device_id_type=MESH,
        )

    def send_plane(step, plane):
        if plane >= planes - 2:

            @pl.when(chip < CHIPS - 1)
            def _():
                to_next(step, plane).start()

        if plane == 0:

            @pl.when(chip > 0)
            def _():
                to_previous(step).start()

        to_side(step, plane).start()

    order = (3, 2, 0, 1)
    for plane in order:
        send_plane(0, plane)

    lanes = lax.broadcasted_iota(jnp.int32, (rows, cols), 1)

    def local_part(step):
        centre = 6.0 + 1.5 * sum(WIND)
        index = last + step
        for plane in range(planes):
            to_side(step, plane).wait_recv()
        for plane in range(planes):
            v = V[index, plane]
            side = side_y[step, plane]
            below = jnp.where(core == 1, side, 0.0)
            above = jnp.where(core == 0, side, 0.0)
            tall = jnp.concatenate([below, v, above], axis=0)
            total = -(RC[plane] + centre) * v
            s = WIND[1]
            total += tall[9 : rows + 9]
            total += (1.0 + 2.0 * s) * tall[7 : rows + 7] - (0.5 * s) * tall[6 : rows + 6]
            s = WIND[2]
            total += jnp.where(lanes < cols - 1, pltpu.roll(v, cols - 1, 1), 0.0)
            total += (1.0 + 2.0 * s) * jnp.where(lanes >= 1, pltpu.roll(v, 1, 1), 0.0)
            total -= (0.5 * s) * jnp.where(lanes >= 2, pltpu.roll(v, 2, 1), 0.0)
            s = WIND[0]
            if plane + 1 < planes:
                total += V[index, plane + 1]
            if plane >= 1:
                total += (1.0 + 2.0 * s) * V[index, plane - 1]
            if plane >= 2:
                total -= (0.5 * s) * V[index, plane - 2]
            W[plane] = total

    def far_part(step):
        s = WIND[0]

        @pl.when(chip > 0)
        def _():
            to_next(step, planes - 2).wait_recv()
            to_next(step, planes - 1).wait_recv()

        @pl.when(chip < CHIPS - 1)
        def _():
            to_previous(step).wait_recv()

        W[0] += (1.0 + 2.0 * s) * low_x[step, 1] - (0.5 * s) * low_x[step, 0]
        W[1] -= (0.5 * s) * low_x[step, 1]
        W[planes - 1] += high_x[step]

    def folded(product):
        half = product[:, : cols // 2] + product[:, cols // 2 :]
        parts = [half[8 * t : 8 * t + 8] for t in range(rows // 8)]
        while len(parts) > 1:
            parts = [a + b for a, b in zip(parts[::2], parts[1::2])]
        return parts[0]

    def project(operands, plane, count, target):
        def one(i):
            v = V[i, plane]
            for offset, w in operands:
                part = folded(v * w)
                target[offset + i] = part if plane == 0 else target[offset + i] + part

        whole = count // 4

        def four(t, carry):
            for q in range(4):
                one(4 * t + q)
            return carry

        lax.fori_loop(0, whole, four, 0)
        for i in range(4 * whole, count):
            one(i)

    def diagonal(shape):
        return lax.broadcasted_iota(jnp.int32, shape, 0) == lax.broadcasted_iota(
            jnp.int32, shape, 1
        )

    def as_row(column, count):
        return jnp.sum(
            jnp.where(diagonal((count, 128)), column, 0.0), axis=0, keepdims=True
        )

    def as_column(row):
        return jnp.sum(
            jnp.where(diagonal((ROWS, 128)), row, 0.0), axis=1, keepdims=True
        )

    def packed(ref, start, count):
        flat = jnp.sum(ref[start : start + count], axis=1)
        return as_row(jnp.sum(flat, axis=1, keepdims=True), count)

    def send_row(n, row):
        row_src[n] = row
        row_all[n, me] = row
        for place in partners(True):
            pltpu.make_async_remote_copy(
                row_src.at[n],
                row_all.at[n, me],
                row_send.at[n],
                row_recv.at[n],
                device_id=device(place),
                device_id_type=MESH,
            ).start()

    def row_bytes(n, sem):
        part = row_all.at[n, pl.ds(0, DEVICES - 1)]
        return pltpu.make_async_copy(part, part, sem.at[n])

    def get_row(n):
        row_bytes(n, row_recv).wait()
        return jnp.sum(row_all[n], axis=0) * inv_cells

    row_id = lax.broadcasted_iota(jnp.int32, (ROWS, 128), 0)
    lane_id = lax.broadcasted_iota(jnp.int32, (ROWS, 128), 1)
    lane_row = lax.broadcasted_iota(jnp.int32, (1, 128), 1)
    row_column = lax.broadcasted_iota(jnp.int32, (ROWS, 1), 0)

    loads[1].wait()
    local_part(0)
    for copy in loads[2:]:
        copy.wait()

    block = 32

    def gram_tile(t, carry):
        plane, tile = lax.div(t, rows // 8), lax.rem(t, rows // 8)
        start = pl.multiple_of(tile * 8, 8)
        v = V[0:block, plane, pl.ds(start, 8), :].reshape(block * 8, cols)
        high = v.astype(jnp.bfloat16)
        rest = v - high.astype(f32)
        low = rest.astype(jnp.bfloat16)
        contract = (((1,), (1,)), ((), ()))
        gram_hh[...] += lax.dot_general(
            high, high, contract, preferred_element_type=f32
        )
        gram_hl[...] += lax.dot_general(high, low, contract, preferred_element_type=f32)
        square = rest * rest
        gram_ll[...] += square[:, : cols // 2] + square[:, cols // 2 :]
        return carry

    lax.fori_loop(0, planes * (rows // 8), gram_tile, 0)
    for plane in range(planes):
        project([(0, V[32, plane]), (ROWS, V[33, plane])], plane, keep, acc_kept)
        project([(2 * ROWS, V[34, plane])], plane, keep, acc_kept)
    for plane in range(planes):
        project([(ROWS, V[last, plane])], plane, keep, acc)

    same = lax.rem(
        lax.broadcasted_iota(jnp.int32, (block * 8, block * 8), 0), 8
    ) == lax.rem(lax.broadcasted_iota(jnp.int32, (block * 8, block * 8), 1), 8)
    pick = (
        lax.div(lax.broadcasted_iota(jnp.int32, (block * 8, 128), 0), 8)
        == lax.broadcasted_iota(jnp.int32, (block * 8, 128), 1)
    ).astype(f32)

    def blocks(ref):
        kept = jnp.where(same, ref[...], 0.0).reshape(block, 8, block * 8)
        return jnp.dot(
            jnp.sum(kept, axis=1),
            pick,
            precision=lax.Precision.HIGHEST,
            preferred_element_type=f32,
        )

    hh, hl = blocks(gram_hh), blocks(gram_hl)
    ll = jnp.sum(
        jnp.sum(gram_ll[...].reshape(block, 8, 128), axis=1), axis=1, keepdims=True
    )
    hh = hh + jnp.where(diagonal((block, 128)), ll, 0.0)

    def dense(matrix):
        total = matrix[0:8]
        for q in range(1, 4):
            total = total + pltpu.roll(matrix[8 * q : 8 * q + 8], block * q, 1)
        return total

    pair_src[0:8] = dense(hh)
    pair_src[8:16] = dense(hl)
    for q in range(3):
        pair_src[16 + q : 17 + q] = packed(acc_kept, ROWS * q, ROWS)
    pair_src[19:32] = jnp.zeros((13, 128), f32)
    to_pair = pltpu.make_async_remote_copy(
        pair_src,
        pair_got,
        gram_send.at[0],
        gram_recv.at[0],
        device_id={"gy": 1 - core, "gx": chip},
        device_id_type=MESH,
    )
    to_pair.start()

    def finish_operator(step, count):
        far_part(step)
        for plane in range(planes):
            project([(0, W[plane])], plane, count, acc)
        send_row(step, packed(acc, 0, 2 * ROWS))

    finish_operator(0, keep)

    to_pair.wait_recv()
    chip_sum = pair_src[...] + pair_got[...]
    half = 16
    mine = jnp.where(core == 0, chip_sum[0:half], chip_sum[half : 2 * half])
    half_src[...] = mine
    half_all[chip] = mine
    for place in partners(False):
        pltpu.make_async_remote_copy(
            half_src,
            half_all.at[chip],
            gram_send.at[1],
            gram_recv.at[1],
            device_id=device(place),
            device_id_type=MESH,
        ).start()

    def half_bytes(sem):
        part = half_all.at[pl.ds(0, CHIPS - 1)]
        return pltpu.make_async_copy(part, part, sem.at[1])

    half_bytes(gram_recv).wait()
    mine = jnp.sum(half_all[...], axis=0) * inv_cells
    pair_src2 = half_got.at[0]
    pair_src2[...] = mine
    swap = pltpu.make_async_remote_copy(
        half_got.at[0],
        half_got.at[1],
        gram_send.at[2],
        gram_recv.at[2],
        device_id={"gy": 1 - core, "gx": chip},
        device_id_type=MESH,
    )
    swap.start()
    swap.wait_recv()
    first_half = jnp.where(core == 0, half_got[0], half_got[1])
    second_half = jnp.where(core == 0, half_got[1], half_got[0])

    def spread(packed_block):
        parts = [packed_block] + [
            pltpu.roll(packed_block, 128 - block * q, 1) for q in range(1, 4)
        ]
        full = jnp.concatenate(parts, axis=0)
        return jnp.where(
            lax.broadcasted_iota(jnp.int32, (block, 128), 1) < block, full, 0.0
        )

    hh, hl = spread(first_half[0:8]), spread(first_half[8:16])
    turned = jnp.concatenate([hl, jnp.zeros((96, 128), f32)], axis=0).T[0:block]
    gram = jnp.concatenate([hh + hl + turned, jnp.zeros((8, 128), f32)], axis=0)
    for q in range(3):
        values = second_half[q : q + 1]
        gram = jnp.where(row_id == block + q, values, gram)
    for q in range(3):
        values = as_column(second_half[q : q + 1])
        gram = jnp.where(lane_id == block + q, values, gram)
    eye = jnp.where(row_id == lane_id, 2.0, 0.0)
    lower = jnp.logical_and(row_id < last, lane_id < last)
    matrix = jnp.where(lower, eye - gram, 0.0)

    scale_row = jnp.ones((1, 128), f32)
    scale_column = jnp.ones((ROWS, 1), f32)
    results = jnp.zeros((ROWS, 128), f32)
    inverse = None
    for step in range(STEPS):
        count = keep + step
        if step > 0:
            local_part(step)
            for plane in range(planes):
                project([(ROWS, V[last + step, plane])], plane, count, acc)
            if step > 1:
                for plane in range(planes):
                    out[step - 2, plane] = V[last + step - 1, plane] * inverse
            finish_operator(step, count)
        sums = get_row(step)
        if step > 0:
            square = jnp.sum(
                jnp.where(lane_row == ROWS + count - 1, sums, 0.0),
                axis=1,
                keepdims=True,
            )
            norm = jnp.sqrt(square + EPSILON)
            inverse = 1.0 / norm
            scale_row = jnp.where(lane_row == count - 1, inverse, scale_row)
            scale_column = jnp.where(row_column == count - 1, inverse, scale_column)
            results = jnp.where(
                jnp.logical_and(row_id == count - 1, lane_id == step - 1), norm, results
            )
            factor = scale_row * inverse
        else:
            factor = scale_row
        valid = lane_row < count
        first = jnp.where(valid, sums * factor, 0.0)
        cross = jnp.where(valid, pltpu.roll(sums, 128 - ROWS, 1) * factor, 0.0)
        cross_column = as_column(cross)
        matrix = jnp.where(row_id == count - 1, eye - cross, matrix)
        matrix = jnp.where(lane_id == count - 1, eye - cross_column, matrix)
        weights = jnp.sum(matrix * first, axis=1, keepdims=True)
        weights = jnp.where(row_column < count, weights, 0.0)
        results = jnp.where(lane_id == step, weights, results)
        hb[...] = jnp.broadcast_to(weights * scale_column, hb.shape)

        for plane in order:
            start = W[plane] if step == 0 else W[plane] * inverse

            def minus(i, total):
                return total - hb[pl.ds(i, 1), :] * V[i, plane]

            def four(t, total):
                for q in range(4):
                    total = minus(4 * t + q, total)
                return total

            total = lax.fori_loop(0, count // 4, four, start)
            for i in range(4 * (count // 4), count):
                total = minus(i, total)
            V[count, plane] = total
            if step + 1 < STEPS:
                send_plane(step + 1, plane)

    total = jnp.zeros((8, 128), f32)
    for plane in range(planes):
        v = V[keep + STEPS - 1, plane]
        total = total + folded(v * v)
    square = jnp.sum(jnp.sum(total, axis=0, keepdims=True), axis=1, keepdims=True)
    send_row(STEPS, jnp.broadcast_to(square, (1, 128)))
    for plane in range(planes):
        out[STEPS - 2, plane] = V[keep + STEPS - 2, plane] * inverse
    sums = get_row(STEPS)
    norm = jnp.sqrt(sums[:, 0:1] + EPSILON)
    inverse = 1.0 / norm
    results = jnp.where(
        jnp.logical_and(row_id == keep + STEPS - 1, lane_id == STEPS - 1), norm, results
    )
    hess[...] = results[:, 0:STEPS]
    for plane in range(planes):
        out[STEPS - 1, plane] = V[keep + STEPS - 1, plane] * inverse

    for step in range(STEPS):

        @pl.when(chip < CHIPS - 1)
        def _():
            to_next(step, planes - 2).wait_send()
            to_next(step, planes - 1).wait_send()

        @pl.when(chip > 0)
        def _():
            to_previous(step).wait_send()

        for plane in range(planes):
            to_side(step, plane).wait_send()
    for n in range(STEPS + 1):
        row_bytes(n, row_send).wait()
    to_pair.wait_send()
    half_bytes(gram_send).wait()
    swap.wait_send()


def body(basis_vectors, reaction):
    keep, planes, rows, cols = basis_vectors.shape
    f32 = jnp.float32
    field = (planes, rows, cols)
    dma = pltpu.SemaphoreType.DMA
    vmem = pltpu.VMEM
    return pl.pallas_call(
        functools.partial(kernel, keep, planes, rows, cols),
        out_shape=(
            jax.ShapeDtypeStruct((STEPS, *field), f32),
            jax.ShapeDtypeStruct((keep + STEPS, STEPS), f32),
        ),
        in_specs=[pl.BlockSpec(memory_space=pl.ANY)] * 2,
        out_specs=(
            pl.BlockSpec(memory_space=pltpu.VMEM),
            pl.BlockSpec(memory_space=pltpu.VMEM),
        ),
        scratch_shapes=[
            vmem((keep + STEPS, *field), f32),
            vmem(field, f32),
            vmem(field, f32),
            vmem((STEPS, 2, rows, cols), f32),
            vmem((STEPS, rows, cols), f32),
            vmem((STEPS, planes, 8, cols), f32),
            vmem((2 * ROWS, 8, 128), f32),
            vmem((3 * ROWS, 8, 128), f32),
            vmem((256, 256), f32),
            vmem((256, 256), f32),
            vmem((256, 128), f32),
            vmem((ROWS, cols), f32),
            vmem((STEPS + 1, 1, 128), f32),
            vmem((STEPS + 1, DEVICES, 1, 128), f32),
            vmem((32, 128), f32),
            vmem((32, 128), f32),
            vmem((16, 128), f32),
            vmem((CHIPS, 16, 128), f32),
            vmem((2, 16, 128), f32),
            dma((9,)),
            dma((STEPS, 3)),
            dma((STEPS, 2)),
            dma((STEPS,)),
            dma((STEPS, planes)),
            dma((STEPS, planes)),
            dma((STEPS + 1,)),
            dma((STEPS + 1,)),
            dma((3,)),
            dma((3,)),
        ],
        compiler_params=pltpu.CompilerParams(
            collective_id=0,
            has_side_effects=True,
            vmem_limit_bytes=48 * 1024 * 1024,
        ),
    )(basis_vectors, reaction)


def solution(mesh):
    return jax.shard_map(
        body,
        mesh=mesh,
        in_specs=(P(None, "gx", "gy", None), P("gx", "gy", None)),
        out_specs=(P(None, "gx", "gy", None), P()),
        check_vma=False,
    )
```

time: 562 us -> 89.8 us (0.16); the launches traced: 552 us -> 89.6 us
  matrix products: 272 us -> 0 us
  starting transfers between devices: 104 us -> 0 us
  Pallas kernels: 0 us -> 86.4 us
  waiting for transfers between devices: 53.9 us -> 0 us
  blocking collectives: 48.8 us -> 0 us
  other arithmetic: 36.2 us -> 0 us
  local copies, waits for them, and re-layouts: 28 us -> 2.57 us
  between operations: 9.69 us -> 0.65 us
    dot_general x21 -> x0, matrix products: 272 us -> none  [the longest x8 126 us: project(): jnp.einsum('kxyz,xyz->k', basis_vectors, image, precision=lax.Precision.H...]
    pallas_call x0 -> x1, Pallas kernels: none -> 86.4 us  [body(): pl.pallas_call(functools.partial(kernel, keep, planes, rows, cols), out_s...]
    all_to_all x9 -> x0, starting transfers between devices: 69.3 us -> none  [copy_for_each(): return lax.all_to_all(copies, axis, split_axis=0, concat_axis=0, tiled=True)]
    all_to_all x9 -> x0, waiting for transfers between devices: 51.6 us -> none  [copy_for_each(): return lax.all_to_all(copies, axis, split_axis=0, concat_axis=0, tiled=True)]
    all_to_all x9 -> x0, blocking collectives: 48.8 us -> none  [copy_for_each(): return lax.all_to_all(copies, axis, split_axis=0, concat_axis=0, tiled=True)]
    ppermute x16 -> x0, starting transfers between devices: 34.5 us -> none  [shifted(): return lax.ppermute(block, axis, route)]
    another operation x16 -> x0, other arithmetic: 11.7 us -> none
    reduce_sum x24 -> x0, other arithmetic: 10.4 us -> none  [the longest x5 6.66 us: project(): extra = [jnp.sum(vector * image)[None] for vector in created]]
  transfers between devices with their start and end apart: 25 -> 0, of which waited for: 11 -> 0; matrix products, arithmetic and copies ran while one was open for 11% -> 0% of each run, Pallas kernels for 0% -> 0%
where the time goes in v1:
time: 89.8 us; the launch traced here: 89.6 us
  Pallas kernels  86.4 us (96%)
  local copies, waits for them, and re-layouts  2.57 us (3%)
    pallas_call x1, Pallas kernels, body(): pl.pallas_call(functools.partial(kernel, keep, planes, rows, cols), out_s...  86.4 us
    unnamed x3, local copies, waits for them, and re-layouts  1.91 us

profile of v1, /device:TPU:1, one launch (start us, length us, event | category | flops | bytes accessed | tf_op | source)
XLA Modules:
  0.0 89.6 jit_solution(4142595286411079385)
XLA Ops:
  0.6 0.0 copy-start
  0.6 0.9 %copy-done = f32[4,64,256]{2,1,0:T(8,128)S(1)} copy-done((f32[4,64,256]{2,1,0:T(8,128)S(1)}, f32[4,64,256]{2,1,0:T(8,128)}, u32[]{:S(2)}) %copy-start) | copy-done | bytes 262168
  1.6 86.4 %shard_map.41 = (f32[4,4,64,256]{3,2,1,0:T(8,128)S(1)}, f32[40,4]{1,0:T(8,128)S(1)}) custom-call(f32[36,4,64,256]{3,2,1,0:T(8,128)} %basis.1, f32[4,64,256]{2,1,0:T(8,128)S(1)} %copy-done), custom_call_target="tpu_custom_call" | custom-call | tf_op jit(solution)/shard_map/pallas_call | solution.py:539
  88.0 0.7 copy.4
  88.7 1.0 %copy.6 = f32[4,4,64,256]{3,2,1,0:T(8,128)} copy(f32[4,4,64,256]{3,2,1,0:T(8,128)S(1)} %get-tuple-element.6) | data formatting | bytes 2097152
Async XLA Ops:
  0.6 1.0 %copy-start = (f32[4,64,256]{2,1,0:T(8,128)S(1)}, f32[4,64,256]{2,1,0:T(8,128)}, u32[]{:S(2)}) copy-start(f32[4,64,256]{2,1,0:T(8,128)} %react.1) | copy-start | bytes 786436

commit v2 on v1

--- a/solution.py
+++ b/solution.py
@@ -53,6 +53,7 @@
     acc_kept,
     gram_hh,
     gram_hl,
+    gram_lh,
     gram_ll,
     hb,
     row_src,
@@ -61,7 +62,7 @@
     pair_got,
     half_src,
     half_all,
-    half_got,
+    swap_buf,
     load_sem,
     x_send,
     low_recv,
@@ -88,12 +89,6 @@
         z, y, x, c = place
         return {"gy": cores[c], "gx": zs[z] + ys[y] + xs[x]}
 
-    barrier = pltpu.get_barrier_semaphore()
-    for place in partners(True):
-        pl.semaphore_signal(
-            barrier, inc=1, device_id=device(place), device_id_type=MESH
-        )
-
     last = keep - 1
     loads = [
         pltpu.make_async_copy(basis.at[last], V.at[last], load_sem.at[0]),
@@ -107,10 +102,17 @@
     for copy in loads:
         copy.start()
 
+    barrier = pltpu.get_barrier_semaphore()
+    for place in partners(True):
+        pl.semaphore_signal(
+            barrier, inc=1, device_id=device(place), device_id_type=MESH
+        )
+
     acc[...] = jnp.zeros(acc.shape, f32)
     acc_kept[...] = jnp.zeros(acc_kept.shape, f32)
     gram_hh[...] = jnp.zeros(gram_hh.shape, f32)
     gram_hl[...] = jnp.zeros(gram_hl.shape, f32)
+    gram_lh[...] = jnp.zeros(gram_lh.shape, f32)
     gram_ll[...] = jnp.zeros(gram_ll.shape, f32)
 
     @pl.when(chip == 0)
@@ -120,9 +122,6 @@
     @pl.when(chip == CHIPS - 1)
     def _():
         high_x[...] = jnp.zeros(high_x.shape, f32)
-
-    loads[0].wait()
-    pl.semaphore_wait(barrier, DEVICES - 1)
 
     def to_next(step, plane):
         return pltpu.make_async_remote_copy(
@@ -172,8 +171,6 @@
         to_side(step, plane).start()
 
     order = (3, 2, 0, 1)
-    for plane in order:
-        send_plane(0, plane)
 
     lanes = lax.broadcasted_iota(jnp.int32, (rows, cols), 1)
 
@@ -205,21 +202,15 @@
                 total -= (0.5 * s) * V[index, plane - 2]
             W[plane] = total
 
-    def far_part(step):
-        s = WIND[0]
-
+    def low_plane(step, plane):
         @pl.when(chip > 0)
         def _():
-            to_next(step, planes - 2).wait_recv()
-            to_next(step, planes - 1).wait_recv()
-
+            to_next(step, plane).wait_recv()
+
+    def high_plane(step):
         @pl.when(chip < CHIPS - 1)
         def _():
             to_previous(step).wait_recv()
-
-        W[0] += (1.0 + 2.0 * s) * low_x[step, 1] - (0.5 * s) * low_x[step, 0]
-        W[1] -= (0.5 * s) * low_x[step, 1]
-        W[planes - 1] += high_x[step]
 
     def folded(product):
         half = product[:, : cols // 2] + product[:, cols // 2 :]
@@ -228,22 +219,22 @@
             parts = [a + b for a, b in zip(parts[::2], parts[1::2])]
         return parts[0]
 
-    def project(operands, plane, count, target):
+    def project(operands, plane, target, first, count, fresh):
         def one(i):
             v = V[i, plane]
             for offset, w in operands:
                 part = folded(v * w)
-                target[offset + i] = part if plane == 0 else target[offset + i] + part
-
-        whole = count // 4
+                target[offset + i] = part if fresh else target[offset + i] + part
+
+        fours = (count - first) // 4
 
         def four(t, carry):
             for q in range(4):
-                one(4 * t + q)
+                one(first + 4 * t + q)
             return carry
 
-        lax.fori_loop(0, whole, four, 0)
-        for i in range(4 * whole, count):
+        lax.fori_loop(0, fours, four, 0)
+        for i in range(first + 4 * fours, count):
             one(i)
 
     def diagonal(shape):
@@ -291,46 +282,69 @@
     lane_row = lax.broadcasted_iota(jnp.int32, (1, 128), 1)
     row_column = lax.broadcasted_iota(jnp.int32, (ROWS, 1), 0)
 
-    loads[1].wait()
-    local_part(0)
+    loads[0].wait()
     for copy in loads[2:]:
         copy.wait()
+    for plane in range(planes):
+        project([(ROWS, V[last, plane])], plane, acc, 0, keep, plane == 0)
+    pl.semaphore_wait(barrier, DEVICES - 1)
+    for plane in order:
+        send_plane(0, plane)
 
     block = 32
-
-    def gram_tile(t, carry):
-        plane, tile = lax.div(t, rows // 8), lax.rem(t, rows // 8)
+    size = block * 8
+    tall = keep * 8
+
+    def gram_tile(tile, carry):
         start = pl.multiple_of(tile * 8, 8)
-        v = V[0:block, plane, pl.ds(start, 8), :].reshape(block * 8, cols)
+        v = jnp.concatenate(
+            [
+                V[0:keep, plane, pl.ds(start, 8), :].reshape(tall, cols)
+                for plane in range(planes)
+            ],
+            axis=1,
+        )
         high = v.astype(jnp.bfloat16)
         rest = v - high.astype(f32)
         low = rest.astype(jnp.bfloat16)
-        contract = (((1,), (1,)), ((), ()))
-        gram_hh[...] += lax.dot_general(
-            high, high, contract, preferred_element_type=f32
-        )
-        gram_hl[...] += lax.dot_general(high, low, contract, preferred_element_type=f32)
-        square = rest * rest
-        gram_ll[...] += square[:, : cols // 2] + square[:, cols // 2 :]
+
+        def product(a, b):
+            return lax.dot_general(
+                a, b, (((1,), (1,)), ((), ())), preferred_element_type=f32
+            )
+
+        gram_hh[...] += product(high, high[0:size])
+        gram_hl[...] += product(high, low[0:size])
+        gram_lh[...] += product(low[size:], high[0:size])
+        square = rest[0:size] * rest[0:size]
+        parts = [square[:, 128 * n : 128 * n + 128] for n in range(planes * cols // 128)]
+        while len(parts) > 1:
+            parts = [a + b for a, b in zip(parts[::2], parts[1::2])]
+        gram_ll[...] += parts[0]
         return carry
 
-    lax.fori_loop(0, planes * (rows // 8), gram_tile, 0)
+    lax.fori_loop(0, rows // 8, gram_tile, 0)
     for plane in range(planes):
-        project([(0, V[32, plane]), (ROWS, V[33, plane])], plane, keep, acc_kept)
-        project([(2 * ROWS, V[34, plane])], plane, keep, acc_kept)
-    for plane in range(planes):
-        project([(ROWS, V[last, plane])], plane, keep, acc)
-
-    same = lax.rem(
-        lax.broadcasted_iota(jnp.int32, (block * 8, block * 8), 0), 8
-    ) == lax.rem(lax.broadcasted_iota(jnp.int32, (block * 8, block * 8), 1), 8)
+        project(
+            [(ROWS * q, V[block + q, plane]) for q in range(3)],
+            plane,
+            acc_kept,
+            block,
+            last,
+            plane == 0,
+        )
+
     pick = (
-        lax.div(lax.broadcasted_iota(jnp.int32, (block * 8, 128), 0), 8)
-        == lax.broadcasted_iota(jnp.int32, (block * 8, 128), 1)
+        lax.div(lax.broadcasted_iota(jnp.int32, (size, 128), 0), 8)
+        == lax.broadcasted_iota(jnp.int32, (size, 128), 1)
     ).astype(f32)
 
     def blocks(ref):
-        kept = jnp.where(same, ref[...], 0.0).reshape(block, 8, block * 8)
+        count = ref.shape[0]
+        same = lax.rem(
+            lax.broadcasted_iota(jnp.int32, (count, size), 0), 8
+        ) == lax.rem(lax.broadcasted_iota(jnp.int32, (count, size), 1), 8)
+        kept = jnp.where(same, ref[...], 0.0).reshape(count // 8, 8, size)
         return jnp.dot(
             jnp.sum(kept, axis=1),
             pick,
@@ -338,51 +352,52 @@
             preferred_element_type=f32,
         )
 
-    hh, hl = blocks(gram_hh), blocks(gram_hl)
+    hh, hl, lh = blocks(gram_hh), blocks(gram_hl), blocks(gram_lh)
     ll = jnp.sum(
         jnp.sum(gram_ll[...].reshape(block, 8, 128), axis=1), axis=1, keepdims=True
     )
-    hh = hh + jnp.where(diagonal((block, 128)), ll, 0.0)
-
-    def dense(matrix):
-        total = matrix[0:8]
-        for q in range(1, 4):
-            total = total + pltpu.roll(matrix[8 * q : 8 * q + 8], block * q, 1)
-        return total
-
-    pair_src[0:8] = dense(hh)
-    pair_src[8:16] = dense(hl)
+    turned = jnp.concatenate([hl[0:block], jnp.zeros((96, 128), f32)], axis=0).T
+    both = hh + hl
+    square = both[0:block] + turned[0:block]
+    square = square + jnp.where(diagonal((block, 128)), ll, 0.0)
+    dense = square[0:8]
+    for q in range(1, 4):
+        dense = dense + pltpu.roll(square[8 * q : 8 * q + 8], block * q, 1)
+    extra = jnp.zeros((1, 128), f32)
     for q in range(3):
-        pair_src[16 + q : 17 + q] = packed(acc_kept, ROWS * q, ROWS)
-    pair_src[19:32] = jnp.zeros((13, 128), f32)
+        exact = packed(acc_kept, ROWS * q, ROWS)
+        values = both[block + q : block + q + 1] + lh[q : q + 1]
+        values = jnp.where(lane_row < block, values, exact)
+        values = jnp.where(lane_row < keep, values, 0.0)
+        extra = extra + (pltpu.roll(values, keep * q, 1) if q else values)
+    pair_src[0:4] = dense[0:4]
+    pair_src[4:5] = extra
+    pair_src[5:8] = jnp.zeros((3, 128), f32)
+    pair_src[8:12] = dense[4:8]
+    pair_src[12:16] = jnp.zeros((4, 128), f32)
+    theirs = pl.ds(pl.multiple_of((1 - core) * 8, 8), 8)
+    partner = {"gy": 1 - core, "gx": chip}
     to_pair = pltpu.make_async_remote_copy(
-        pair_src,
+        pair_src.at[theirs],
         pair_got,
         gram_send.at[0],
         gram_recv.at[0],
-        device_id={"gy": 1 - core, "gx": chip},
+        device_id=partner,
         device_id_type=MESH,
     )
     to_pair.start()
-
-    def finish_operator(step, count):
-        far_part(step)
-        for plane in range(planes):
-            project([(0, W[plane])], plane, count, acc)
-        send_row(step, packed(acc, 0, 2 * ROWS))
-
-    finish_operator(0, keep)
-
+    loads[1].wait()
+    local_part(0)
+    project([(0, W[2])], 2, acc, 0, keep, True)
     to_pair.wait_recv()
-    chip_sum = pair_src[...] + pair_got[...]
-    half = 16
-    mine = jnp.where(core == 0, chip_sum[0:half], chip_sum[half : 2 * half])
+    mine = jnp.where(core == 0, pair_src[0:8], pair_src[8:16]) + pair_got[...]
+    used = pl.ds(0, 5)
     half_src[...] = mine
-    half_all[chip] = mine
+    half_all[chip, 0:5] = mine[0:5]
     for place in partners(False):
         pltpu.make_async_remote_copy(
-            half_src,
-            half_all.at[chip],
+            half_src.at[used],
+            half_all.at[chip, used],
             gram_send.at[1],
             gram_recv.at[1],
             device_id=device(place),
@@ -390,44 +405,51 @@
         ).start()
 
     def half_bytes(sem):
-        part = half_all.at[pl.ds(0, CHIPS - 1)]
+        part = half_all.at[pl.ds(0, CHIPS - 1), used]
         return pltpu.make_async_copy(part, part, sem.at[1])
 
+    def finish_operator(step, count):
+        s = WIND[0]
+        high_plane(step)
+        W[3] += high_x[step]
+        project([(0, W[3])], 3, acc, 0, count, False)
+        low_plane(step, planes - 1)
+        W[1] -= (0.5 * s) * low_x[step, 1]
+        project([(0, W[1])], 1, acc, 0, count, False)
+        low_plane(step, planes - 2)
+        W[0] += (1.0 + 2.0 * s) * low_x[step, 1] - (0.5 * s) * low_x[step, 0]
+        project([(0, W[0])], 0, acc, 0, count, False)
+        send_row(step, packed(acc, 0, 2 * ROWS))
+
+    finish_operator(0, keep)
+
     half_bytes(gram_recv).wait()
-    mine = jnp.sum(half_all[...], axis=0) * inv_cells
-    pair_src2 = half_got.at[0]
-    pair_src2[...] = mine
+    swap_buf[0] = jnp.sum(half_all[:, 0:5], axis=0) * inv_cells
     swap = pltpu.make_async_remote_copy(
-        half_got.at[0],
-        half_got.at[1],
+        swap_buf.at[0],
+        swap_buf.at[1],
         gram_send.at[2],
         gram_recv.at[2],
-        device_id={"gy": 1 - core, "gx": chip},
+        device_id=partner,
         device_id_type=MESH,
     )
     swap.start()
     swap.wait_recv()
-    first_half = jnp.where(core == 0, half_got[0], half_got[1])
-    second_half = jnp.where(core == 0, half_got[1], half_got[0])
-
-    def spread(packed_block):
-        parts = [packed_block] + [
-            pltpu.roll(packed_block, 128 - block * q, 1) for q in range(1, 4)
-        ]
-        full = jnp.concatenate(parts, axis=0)
-        return jnp.where(
-            lax.broadcasted_iota(jnp.int32, (block, 128), 1) < block, full, 0.0
-        )
-
-    hh, hl = spread(first_half[0:8]), spread(first_half[8:16])
-    turned = jnp.concatenate([hl, jnp.zeros((96, 128), f32)], axis=0).T[0:block]
-    gram = jnp.concatenate([hh + hl + turned, jnp.zeros((8, 128), f32)], axis=0)
+    even = jnp.where(core == 0, swap_buf[0], swap_buf[1])
+    odd = jnp.where(core == 0, swap_buf[1], swap_buf[0])
+    dense = jnp.concatenate([even[0:4], odd[0:4]], axis=0)
+    parts = [dense] + [pltpu.roll(dense, 128 - block * q, 1) for q in range(1, 4)]
+    square = jnp.concatenate(parts, axis=0)
+    square = jnp.where(
+        lax.broadcasted_iota(jnp.int32, (block, 128), 1) < block, square, 0.0
+    )
+    gram = jnp.concatenate([square, jnp.zeros((8, 128), f32)], axis=0)
+    extra = even[4:5]
+    values = [extra] + [pltpu.roll(extra, 128 - keep * q, 1) for q in range(1, 3)]
     for q in range(3):
-        values = second_half[q : q + 1]
-        gram = jnp.where(row_id == block + q, values, gram)
+        gram = jnp.where(row_id == block + q, values[q], gram)
     for q in range(3):
-        values = as_column(second_half[q : q + 1])
-        gram = jnp.where(lane_id == block + q, values, gram)
+        gram = jnp.where(lane_id == block + q, as_column(values[q]), gram)
     eye = jnp.where(row_id == lane_id, 2.0, 0.0)
     lower = jnp.logical_and(row_id < last, lane_id < last)
     matrix = jnp.where(lower, eye - gram, 0.0)
@@ -440,8 +462,11 @@
         count = keep + step
         if step > 0:
             local_part(step)
-            for plane in range(planes):
-                project([(ROWS, V[last + step, plane])], plane, count, acc)
+            project(
+                [(0, W[2]), (ROWS, V[last + step, 2])], 2, acc, 0, count, True
+            )
+            for plane in (3, 1, 0):
+                project([(ROWS, V[last + step, plane])], plane, acc, 0, count, False)
             if step > 1:
                 for plane in range(planes):
                     out[step - 2, plane] = V[last + step - 1, plane] * inverse
@@ -542,7 +567,7 @@
             jax.ShapeDtypeStruct((STEPS, *field), f32),
             jax.ShapeDtypeStruct((keep + STEPS, STEPS), f32),
         ),
-        in_specs=[pl.BlockSpec(memory_space=pl.ANY)] * 2,
+        in_specs=[pl.BlockSpec(memory_space=pltpu.HBM)] * 2,
         out_specs=(
             pl.BlockSpec(memory_space=pltpu.VMEM),
             pl.BlockSpec(memory_space=pltpu.VMEM),
@@ -556,17 +581,18 @@
             vmem((STEPS, planes, 8, cols), f32),
             vmem((2 * ROWS, 8, 128), f32),
             vmem((3 * ROWS, 8, 128), f32),
-            vmem((256, 256), f32),
-            vmem((256, 256), f32),
+            vmem((8 * keep, 256), f32),
+            vmem((8 * keep, 256), f32),
+            vmem((8 * keep - 256, 256), f32),
             vmem((256, 128), f32),
             vmem((ROWS, cols), f32),
             vmem((STEPS + 1, 1, 128), f32),
             vmem((STEPS + 1, DEVICES, 1, 128), f32),
-            vmem((32, 128), f32),
-            vmem((32, 128), f32),
             vmem((16, 128), f32),
-            vmem((CHIPS, 16, 128), f32),
-            vmem((2, 16, 128), f32),
+            vmem((8, 128), f32),
+            vmem((8, 128), f32),
+            vmem((CHIPS, 8, 128), f32),
+            vmem((2, 5, 128), f32),
             dma((9,)),
             dma((STEPS, 3)),
             dma((STEPS, 2)),
@@ -581,7 +607,7 @@
         compiler_params=pltpu.CompilerParams(
             collective_id=0,
             has_side_effects=True,
-            vmem_limit_bytes=48 * 1024 * 1024,
+            vmem_limit_bytes=65890000,
         ),
     )(basis_vectors, reaction)
 

time: 89.8 us -> 78 us (0.87)
  Pallas kernels: 86.4 us -> 73.5 us
  local copies, waits for them, and re-layouts: 2.57 us -> 3.67 us
    pallas_call x1, Pallas kernels: 86.4 us -> 73.5 us  [body(): pl.pallas_call(functools.partial(kernel, keep, planes, rows, cols), out_s...]
    unnamed x3 -> x1, local copies, waits for them, and re-layouts: 1.91 us -> 2.29 us
where the time goes in v2:
time: 78 us; the launch traced here: 77.8 us
  Pallas kernels  73.5 us (94%)
  local copies, waits for them, and re-layouts  3.67 us (5%)
    pallas_call x1, Pallas kernels, body(): pl.pallas_call(functools.partial(kernel, keep, planes, rows, cols), out_s...  73.5 us
    unnamed x1, local copies, waits for them, and re-layouts  2.29 us

profile of v2, /device:TPU:1, one launch (start us, length us, event | category | flops | bytes accessed | tf_op | source)
XLA Modules:
  0.0 77.8 jit_solution(1247577793686525740)
XLA Ops:
  0.6 73.5 %shard_map.41 = (f32[4,4,64,256]{3,2,1,0:T(8,128)}, f32[40,4]{1,0:T(8,128)}) custom-call(f32[36,4,64,256]{3,2,1,0:T(8,128)} %basis.1, f32[4,64,256]{2,1,0:T(8,128)} %react.1), custom_call_target="tpu_custom_call" | custom-call | tf_op jit(solution)/shard_map/pallas_call | solution.py:564
  74.1 1.4 %copy.4 = f32[40,4]{0,1:T(4,128)} copy(f32[40,4]{1,0:T(8,128)} %get-tuple-element.3) | data formatting | bytes 1280 | tf_op jit(solution)/shard_map/pallas_call | solution.py:564
  75.5 2.3 %copy.6 = f32[4,4,64,256]{3,2,1,0:T(8,128)} copy(f32[4,4,64,256]{3,2,1,0:T(8,128)} %get-tuple-element.6) | data formatting | bytes 2097152

commit v3 on v2

--- a/solution.py
+++ b/solution.py
@@ -456,7 +456,9 @@
 
     scale_row = jnp.ones((1, 128), f32)
     scale_column = jnp.ones((ROWS, 1), f32)
-    results = jnp.zeros((ROWS, 128), f32)
+    results = jnp.zeros((8, 128), f32)
+    row_8 = lax.broadcasted_iota(jnp.int32, (8, 128), 0)
+    lane_8 = lax.broadcasted_iota(jnp.int32, (8, 128), 1)
     inverse = None
     for step in range(STEPS):
         count = keep + step
@@ -483,7 +485,7 @@
             scale_row = jnp.where(lane_row == count - 1, inverse, scale_row)
             scale_column = jnp.where(row_column == count - 1, inverse, scale_column)
             results = jnp.where(
-                jnp.logical_and(row_id == count - 1, lane_id == step - 1), norm, results
+                jnp.logical_and(row_8 == step - 1, lane_8 == count - 1), norm, results
             )
             factor = scale_row * inverse
         else:
@@ -496,7 +498,6 @@
         matrix = jnp.where(lane_id == count - 1, eye - cross_column, matrix)
         weights = jnp.sum(matrix * first, axis=1, keepdims=True)
         weights = jnp.where(row_column < count, weights, 0.0)
-        results = jnp.where(lane_id == step, weights, results)
         hb[...] = jnp.broadcast_to(weights * scale_column, hb.shape)
 
         for plane in order:
@@ -516,6 +517,7 @@
             V[count, plane] = total
             if step + 1 < STEPS:
                 send_plane(step + 1, plane)
+        results = jnp.where(row_8 == step, as_row(weights, ROWS), results)
 
     total = jnp.zeros((8, 128), f32)
     for plane in range(planes):
@@ -529,9 +531,9 @@
     norm = jnp.sqrt(sums[:, 0:1] + EPSILON)
     inverse = 1.0 / norm
     results = jnp.where(
-        jnp.logical_and(row_id == keep + STEPS - 1, lane_id == STEPS - 1), norm, results
+        jnp.logical_and(row_8 == STEPS - 1, lane_8 == keep + STEPS - 1), norm, results
     )
-    hess[...] = results[:, 0:STEPS]
+    hess[...] = results[0:STEPS, 0:ROWS]
     for plane in range(planes):
         out[STEPS - 1, plane] = V[keep + STEPS - 1, plane] * inverse
 
@@ -555,17 +557,29 @@
     swap.wait_send()
 
 
+def put_out(vectors, columns, vectors_out, columns_out, sem):
+    copies = [
+        pltpu.make_async_copy(vectors, vectors_out, sem.at[0]),
+        pltpu.make_async_copy(columns, columns_out, sem.at[1]),
+    ]
+    for copy in copies:
+        copy.start()
+    for copy in copies:
+        copy.wait()
+
+
 def body(basis_vectors, reaction):
     keep, planes, rows, cols = basis_vectors.shape
     f32 = jnp.float32
     field = (planes, rows, cols)
     dma = pltpu.SemaphoreType.DMA
     vmem = pltpu.VMEM
-    return pl.pallas_call(
+    reaction = pltpu.with_memory_space_constraint(reaction, pltpu.HBM)
+    vectors, columns = pl.pallas_call(
         functools.partial(kernel, keep, planes, rows, cols),
         out_shape=(
             jax.ShapeDtypeStruct((STEPS, *field), f32),
-            jax.ShapeDtypeStruct((keep + STEPS, STEPS), f32),
+            jax.ShapeDtypeStruct((STEPS, keep + STEPS), f32),
         ),
         in_specs=[pl.BlockSpec(memory_space=pltpu.HBM)] * 2,
         out_specs=(
@@ -607,9 +621,19 @@
         compiler_params=pltpu.CompilerParams(
             collective_id=0,
             has_side_effects=True,
-            vmem_limit_bytes=65890000,
+            vmem_limit_bytes=48 * 1024 * 1024,
         ),
     )(basis_vectors, reaction)
+    shapes = (vectors, columns)
+    new_vectors, rows_out = pl.pallas_call(
+        put_out,
+        out_shape=tuple(jax.ShapeDtypeStruct(a.shape, f32) for a in shapes),
+        in_specs=[pl.BlockSpec(memory_space=pltpu.VMEM)] * 2,
+        out_specs=(pl.BlockSpec(memory_space=pl.ANY),) * 2,
+        scratch_shapes=[dma((2,))],
+        compiler_params=pltpu.CompilerParams(vmem_limit_bytes=4 * 1024 * 1024),
+    )(vectors, columns)
+    return new_vectors, rows_out.T
 
 
 def solution(mesh):

time: 78 us -> 74.1 us (0.950)
  local copies, waits for them, and re-layouts: 3.67 us -> 0 us
    unnamed x1 -> x0, local copies, waits for them, and re-layouts: 2.29 us -> none
    pallas_call x1 -> x0, local copies, waits for them, and re-layouts: 1.38 us -> none  [body(): pl.pallas_call(functools.partial(kernel, keep, planes, rows, cols), out_s...]
    pallas_call x1, Pallas kernels: 73.5 us -> 72.4 us  [body(): pl.pallas_call(functools.partial(kernel, keep, planes, rows, cols), out_s...]
    pallas_call x0 -> x1, Pallas kernels: none -> 0.99 us  [body(): pl.pallas_call(put_out, out_shape=tuple((jax.ShapeDtypeStruct(a.shape, f3...]
where the time goes in v3:
time: 74.1 us; the launch traced here: 74 us
  Pallas kernels  73.3 us (99%)
    pallas_call x1, Pallas kernels, body(): pl.pallas_call(functools.partial(kernel, keep, planes, rows, cols), out_s...  72.4 us

profile of v3, /device:TPU:1, one launch (start us, length us, event | category | flops | bytes accessed | tf_op | source)
XLA Modules:
  0.0 74.0 jit_solution(14386490672180610582)
XLA Ops:
  0.6 72.4 %shard_map.41 = (f32[4,4,64,256]{3,2,1,0:T(8,128)S(1)}, f32[4,40]{1,0:T(4,128)S(1)}) custom-call(f32[36,4,64,256]{3,2,1,0:T(8,128)} %basis.1, f32[4,64,256]{2,1,0:T(8,128)} %react.1), custom_call_target="tpu_custom_call" | custom-call | tf_op jit(solution)/shard_map/pallas_call | solution.py:578
  73.0 1.0 %shard_map.42 = (f32[4,4,64,256]{3,2,1,0:T(8,128)}, f32[4,40]{1,0:T(4,128)}) custom-call(f32[4,4,64,256]{3,2,1,0:T(8,128)S(1)} %get-tuple-element.6.vectors, f32[4,40]{1,0:T(4,128)S(1)} %get-tuple-element.7.columns), custom_call_target="tpu_custom_call" | custom-call | tf_op jit(solution)/shard_map/pallas_call | solution.py:628

commit v4 on v3

--- a/solution.py
+++ b/solution.py
@@ -15,6 +15,7 @@
 CHIPS = 64
 DEVICES = 128
 ROWS = 40
+PIECES = {2: 4, 3: 2}
 
 
 def hops(delta):
@@ -64,6 +65,7 @@
     half_all,
     swap_buf,
     load_sem,
+    next_send,
     x_send,
     low_recv,
     high_recv,
@@ -123,12 +125,17 @@
     def _():
         high_x[...] = jnp.zeros(high_x.shape, f32)
 
-    def to_next(step, plane):
+    def piece(plane, part):
+        size = rows // PIECES[plane]
+        return pl.ds(part * size, size)
+
+    def to_next(step, plane, part):
+        place, where = plane - (planes - 2), piece(plane, part)
         return pltpu.make_async_remote_copy(
-            V.at[last + step, plane],
-            low_x.at[step, plane - (planes - 2)],
-            x_send.at[step, plane - (planes - 2)],
-            low_recv.at[step, plane - (planes - 2)],
+            V.at[last + step, plane, where],
+            low_x.at[step, place, where],
+            next_send.at[step, place, part],
+            low_recv.at[step, place, part],
             device_id={"gy": core, "gx": lax.rem(chip + 1, CHIPS)},
             device_id_type=MESH,
         )
@@ -137,7 +144,7 @@
         return pltpu.make_async_remote_copy(
             V.at[last + step, 0],
             high_x.at[step],
-            x_send.at[step, 2],
+            x_send.at[step],
             high_recv.at[step],
             device_id={"gy": core, "gx": lax.rem(chip + CHIPS - 1, CHIPS)},
             device_id_type=MESH,
@@ -155,13 +162,12 @@
             device_id_type=MESH,
         )
 
-    def send_plane(step, plane):
-        if plane >= planes - 2:
-
-            @pl.when(chip < CHIPS - 1)
-            def _():
-                to_next(step, plane).start()
-
+    def send_piece(step, plane, part):
+        @pl.when(chip < CHIPS - 1)
+        def _():
+            to_next(step, plane, part).start()
+
+    def send_rest(step, plane):
         if plane == 0:
 
             @pl.when(chip > 0)
@@ -170,7 +176,13 @@
 
         to_side(step, plane).start()
 
-    order = (3, 2, 0, 1)
+    def send_plane(step, plane):
+        if plane >= planes - 2:
+            for part in range(PIECES[plane]):
+                send_piece(step, plane, part)
+        send_rest(step, plane)
+
+    order = (3, 0, 2, 1)
 
     lanes = lax.broadcasted_iota(jnp.int32, (rows, cols), 1)
 
@@ -202,10 +214,10 @@
                 total -= (0.5 * s) * V[index, plane - 2]
             W[plane] = total
 
-    def low_plane(step, plane):
+    def low_plane(step, plane, part):
         @pl.when(chip > 0)
         def _():
-            to_next(step, plane).wait_recv()
+            to_next(step, plane, part).wait_recv()
 
     def high_plane(step):
         @pl.when(chip < CHIPS - 1)
@@ -214,14 +226,14 @@
 
     def folded(product):
         half = product[:, : cols // 2] + product[:, cols // 2 :]
-        parts = [half[8 * t : 8 * t + 8] for t in range(rows // 8)]
+        parts = [half[8 * t : 8 * t + 8] for t in range(product.shape[0] // 8)]
         while len(parts) > 1:
             parts = [a + b for a, b in zip(parts[::2], parts[1::2])]
         return parts[0]
 
-    def project(operands, plane, target, first, count, fresh):
+    def project(operands, plane, target, first, count, fresh, where=slice(None)):
         def one(i):
-            v = V[i, plane]
+            v = V[i, plane, where]
             for offset, w in operands:
                 part = folded(v * w)
                 target[offset + i] = part if fresh else target[offset + i] + part
@@ -285,12 +297,6 @@
     loads[0].wait()
     for copy in loads[2:]:
         copy.wait()
-    for plane in range(planes):
-        project([(ROWS, V[last, plane])], plane, acc, 0, keep, plane == 0)
-    pl.semaphore_wait(barrier, DEVICES - 1)
-    for plane in order:
-        send_plane(0, plane)
-
     block = 32
     size = block * 8
     tall = keep * 8
@@ -323,7 +329,12 @@
         gram_ll[...] += parts[0]
         return carry
 
-    lax.fori_loop(0, rows // 8, gram_tile, 0)
+    early = 2
+    lax.fori_loop(0, early, gram_tile, 0)
+    pl.semaphore_wait(barrier, DEVICES - 1)
+    for plane in order:
+        send_plane(0, plane)
+    lax.fori_loop(early, rows // 8, gram_tile, 0)
     for plane in range(planes):
         project(
             [(ROWS * q, V[block + q, plane]) for q in range(3)],
@@ -339,26 +350,29 @@
         == lax.broadcasted_iota(jnp.int32, (size, 128), 1)
     ).astype(f32)
 
-    def blocks(ref):
-        count = ref.shape[0]
+    def blocks(matrix):
+        count = matrix.shape[0]
         same = lax.rem(
             lax.broadcasted_iota(jnp.int32, (count, size), 0), 8
         ) == lax.rem(lax.broadcasted_iota(jnp.int32, (count, size), 1), 8)
-        kept = jnp.where(same, ref[...], 0.0).reshape(count // 8, 8, size)
-        return jnp.dot(
-            jnp.sum(kept, axis=1),
-            pick,
-            precision=lax.Precision.HIGHEST,
-            preferred_element_type=f32,
-        )
-
-    hh, hl, lh = blocks(gram_hh), blocks(gram_hl), blocks(gram_lh)
+        kept = jnp.where(same, matrix, 0.0).reshape(count // 8, 8, size)
+        return jnp.sum(kept, axis=1)
+
+    stacked = jnp.concatenate(
+        [
+            blocks(0.5 * gram_hh[0:size] + gram_hl[0:size]),
+            blocks(gram_hh[size:] + gram_hl[size:] + gram_lh[...]),
+        ],
+        axis=0,
+    )
+    inner = jnp.dot(
+        stacked, pick, precision=lax.Precision.HIGHEST, preferred_element_type=f32
+    )
     ll = jnp.sum(
         jnp.sum(gram_ll[...].reshape(block, 8, 128), axis=1), axis=1, keepdims=True
     )
-    turned = jnp.concatenate([hl[0:block], jnp.zeros((96, 128), f32)], axis=0).T
-    both = hh + hl
-    square = both[0:block] + turned[0:block]
+    turned = jnp.concatenate([inner[0:block], jnp.zeros((96, 128), f32)], axis=0).T
+    square = inner[0:block] + turned[0:block]
     square = square + jnp.where(diagonal((block, 128)), ll, 0.0)
     dense = square[0:8]
     for q in range(1, 4):
@@ -366,7 +380,7 @@
     extra = jnp.zeros((1, 128), f32)
     for q in range(3):
         exact = packed(acc_kept, ROWS * q, ROWS)
-        values = both[block + q : block + q + 1] + lh[q : q + 1]
+        values = inner[block + q : block + q + 1]
         values = jnp.where(lane_row < block, values, exact)
         values = jnp.where(lane_row < keep, values, 0.0)
         extra = extra + (pltpu.roll(values, keep * q, 1) if q else values)
@@ -388,7 +402,7 @@
     to_pair.start()
     loads[1].wait()
     local_part(0)
-    project([(0, W[2])], 2, acc, 0, keep, True)
+    project([(0, W[2]), (ROWS, V[last, 2])], 2, acc, 0, keep, True)
     to_pair.wait_recv()
     mine = jnp.where(core == 0, pair_src[0:8], pair_src[8:16]) + pair_got[...]
     used = pl.ds(0, 5)
@@ -404,6 +418,9 @@
             device_id_type=MESH,
         ).start()
 
+    for plane in (3, 1, 0):
+        project([(ROWS, V[last, plane])], plane, acc, 0, keep, False)
+
     def half_bytes(sem):
         part = half_all.at[pl.ds(0, CHIPS - 1), used]
         return pltpu.make_async_copy(part, part, sem.at[1])
@@ -413,12 +430,16 @@
         high_plane(step)
         W[3] += high_x[step]
         project([(0, W[3])], 3, acc, 0, count, False)
-        low_plane(step, planes - 1)
+        for part in range(PIECES[3]):
+            low_plane(step, planes - 1, part)
         W[1] -= (0.5 * s) * low_x[step, 1]
         project([(0, W[1])], 1, acc, 0, count, False)
-        low_plane(step, planes - 2)
-        W[0] += (1.0 + 2.0 * s) * low_x[step, 1] - (0.5 * s) * low_x[step, 0]
-        project([(0, W[0])], 0, acc, 0, count, False)
+        W[0] += (1.0 + 2.0 * s) * low_x[step, 1]
+        for part in range(PIECES[2]):
+            where = piece(planes - 2, part)
+            low_plane(step, planes - 2, part)
+            W[0, where] -= (0.5 * s) * low_x[step, 0, where]
+            project([(0, W[0, where])], 0, acc, 0, count, False, where)
         send_row(step, packed(acc, 0, 2 * ROWS))
 
     finish_operator(0, keep)
@@ -500,11 +521,13 @@
         weights = jnp.where(row_column < count, weights, 0.0)
         hb[...] = jnp.broadcast_to(weights * scale_column, hb.shape)
 
-        for plane in order:
-            start = W[plane] if step == 0 else W[plane] * inverse
+        def combine(plane, where):
+            start = W[plane, where]
+            if step > 0:
+                start = start * inverse
 
             def minus(i, total):
-                return total - hb[pl.ds(i, 1), :] * V[i, plane]
+                return total - hb[pl.ds(i, 1), :] * V[i, plane, where]
 
             def four(t, total):
                 for q in range(4):
@@ -514,9 +537,18 @@
             total = lax.fori_loop(0, count // 4, four, start)
             for i in range(4 * (count // 4), count):
                 total = minus(i, total)
-            V[count, plane] = total
-            if step + 1 < STEPS:
-                send_plane(step + 1, plane)
+            V[count, plane, where] = total
+
+        more = step + 1 < STEPS
+        for plane in order:
+            if more and plane >= planes - 2:
+                for part in range(PIECES[plane]):
+                    combine(plane, piece(plane, part))
+                    send_piece(step + 1, plane, part)
+            else:
+                combine(plane, slice(None))
+            if more:
+                send_rest(step + 1, plane)
         results = jnp.where(row_8 == step, as_row(weights, ROWS), results)
 
     total = jnp.zeros((8, 128), f32)
@@ -541,8 +573,9 @@
 
         @pl.when(chip < CHIPS - 1)
         def _():
-            to_next(step, planes - 2).wait_send()
-            to_next(step, planes - 1).wait_send()
+            for plane in (planes - 2, planes - 1):
+                for part in range(PIECES[plane]):
+                    to_next(step, plane, part).wait_send()
 
         @pl.when(chip > 0)
         def _():
@@ -608,8 +641,9 @@
             vmem((CHIPS, 8, 128), f32),
             vmem((2, 5, 128), f32),
             dma((9,)),
-            dma((STEPS, 3)),
-            dma((STEPS, 2)),
+            dma((STEPS, 2, 4)),
+            dma((STEPS,)),
+            dma((STEPS, 2, 4)),
             dma((STEPS,)),
             dma((STEPS, planes)),
             dma((STEPS, planes)),

time: 74.1 us -> 72.5 us (0.978)
  Pallas kernels: 73.3 us -> 71.8 us
    pallas_call x1, Pallas kernels: 72.4 us -> 70.8 us  [body(): pl.pallas_call(functools.partial(kernel, keep, planes, rows, cols), out_s...]
where the time goes in v4:
time: 72.5 us; the launch traced here: 72.4 us
  Pallas kernels  71.8 us (99%)
    pallas_call x1, Pallas kernels, body(): pl.pallas_call(functools.partial(kernel, keep, planes, rows, cols), out_s...  70.8 us

profile of v4, /device:TPU:1, one launch (start us, length us, event | category | flops | bytes accessed | tf_op | source)
XLA Modules:
  0.0 72.4 jit_solution(9204101537212108115)
XLA Ops:
  0.6 70.8 %shard_map.41 = (f32[4,4,64,256]{3,2,1,0:T(8,128)S(1)}, f32[4,40]{1,0:T(4,128)S(1)}) custom-call(f32[36,4,64,256]{3,2,1,0:T(8,128)} %basis.1, f32[4,64,256]{2,1,0:T(8,128)} %react.1), custom_call_target="tpu_custom_call" | custom-call | tf_op jit(solution)/shard_map/pallas_call | solution.py:611
  71.4 1.0 %shard_map.42 = (f32[4,4,64,256]{3,2,1,0:T(8,128)}, f32[4,40]{1,0:T(4,128)}) custom-call(f32[4,4,64,256]{3,2,1,0:T(8,128)S(1)} %get-tuple-element.6.vectors, f32[4,40]{1,0:T(4,128)S(1)} %get-tuple-element.7.columns), custom_call_target="tpu_custom_call" | custom-call | tf_op jit(solution)/shard_map/pallas_call | solution.py:662

commit v5 on v4

--- a/solution.py
+++ b/solution.py
@@ -15,7 +15,7 @@
 CHIPS = 64
 DEVICES = 128
 ROWS = 40
-PIECES = {2: 4, 3: 2}
+PIECES = {2: 4, 3: 4}
 
 
 def hops(delta):
@@ -31,7 +31,7 @@
         for c in range(2 if with_core else 1)
     ]
     return sorted(
-        [p for p in places if any(p)], key=lambda p: (-hops(p), p[2], p[1], p[0])
+        [p for p in places if any(p)], key=lambda p: (-2 * hops(p) - p[3], p[0], p[1], p[2])
     )
 
 

time: 72.5 us -> 72.3 us (level)
  no operation moved by 1% of the time
where the time goes in v5:
time: 72.3 us; the launch traced here: 72.2 us
  Pallas kernels  71.6 us (99%)
    pallas_call x1, Pallas kernels, body(): pl.pallas_call(functools.partial(kernel, keep, planes, rows, cols), out_s...  70.6 us

profile of v5, /device:TPU:1, one launch (start us, length us, event | category | flops | bytes accessed | tf_op | source)
XLA Modules:
  0.0 72.2 jit_solution(13759825683716487340)
XLA Ops:
  0.6 70.6 %shard_map.41 = (f32[4,4,64,256]{3,2,1,0:T(8,128)S(1)}, f32[4,40]{1,0:T(4,128)S(1)}) custom-call(f32[36,4,64,256]{3,2,1,0:T(8,128)} %basis.1, f32[4,64,256]{2,1,0:T(8,128)} %react.1), custom_call_target="tpu_custom_call" | custom-call | tf_op jit(solution)/shard_map/pallas_call | solution.py:611
  71.2 1.0 %shard_map.42 = (f32[4,4,64,256]{3,2,1,0:T(8,128)}, f32[4,40]{1,0:T(4,128)}) custom-call(f32[4,4,64,256]{3,2,1,0:T(8,128)S(1)} %get-tuple-element.6.vectors, f32[4,40]{1,0:T(4,128)S(1)} %get-tuple-element.7.columns), custom_call_target="tpu_custom_call" | custom-call | tf_op jit(solution)/shard_map/pallas_call | solution.py:662

commit v6 on v5

--- a/solution.py
+++ b/solution.py
@@ -513,8 +513,11 @@
             factor = scale_row
         valid = lane_row < count
         first = jnp.where(valid, sums * factor, 0.0)
-        cross = jnp.where(valid, pltpu.roll(sums, 128 - ROWS, 1) * factor, 0.0)
-        cross_column = as_column(cross)
+        moved = jnp.where(valid, pltpu.roll(sums, 128 - ROWS, 1), 0.0)
+        cross = moved * factor
+        cross_column = as_column(moved) * scale_column
+        if step > 0:
+            cross_column = cross_column * inverse
         matrix = jnp.where(row_id == count - 1, eye - cross, matrix)
         matrix = jnp.where(lane_id == count - 1, eye - cross_column, matrix)
         weights = jnp.sum(matrix * first, axis=1, keepdims=True)

time: 72.3 us -> 72.2 us (level)
  no operation moved by 1% of the time
where the time goes in v6:
time: 72.2 us; the launch traced here: 72.1 us
  Pallas kernels  71.5 us (99%)
    pallas_call x1, Pallas kernels, body(): pl.pallas_call(functools.partial(kernel, keep, planes, rows, cols), out_s...  70.5 us

profile of v6, /device:TPU:1, one launch (start us, length us, event | category | flops | bytes accessed | tf_op | source)
XLA Modules:
  0.0 72.1 jit_solution(18373709736948527255)
XLA Ops:
  0.6 70.5 %shard_map.41 = (f32[4,4,64,256]{3,2,1,0:T(8,128)S(1)}, f32[4,40]{1,0:T(4,128)S(1)}) custom-call(f32[36,4,64,256]{3,2,1,0:T(8,128)} %basis.1, f32[4,64,256]{2,1,0:T(8,128)} %react.1), custom_call_target="tpu_custom_call" | custom-call | tf_op jit(solution)/shard_map/pallas_call | solution.py:614
  71.1 1.0 %shard_map.42 = (f32[4,4,64,256]{3,2,1,0:T(8,128)}, f32[4,40]{1,0:T(4,128)}) custom-call(f32[4,4,64,256]{3,2,1,0:T(8,128)S(1)} %get-tuple-element.6.vectors, f32[4,40]{1,0:T(4,128)S(1)} %get-tuple-element.7.columns), custom_call_target="tpu_custom_call" | custom-call | tf_op jit(solution)/shard_map/pallas_call | solution.py:665
